TPU v7x, 32 devices: a whole 2x2x4 slice. The times are simulated.
32 devices in a mesh: dp: 4 (over x, core), pipe: 4 (over z), tensor: 2 (over y).
Axes of the slice: x: 2, y: 2, z: 4, core: 2. Of those that a mesh axis runs over, the one named last changes fastest.
Arguments:
- support_tokens: int32 [32, 32], P(('dp', 'pipe')), may hold values from 0 to 64127
- support_lengths: int32 [32], P(('dp', 'pipe')), may hold values from 1 to 32
- support_labels: int32 [32, 1], P(('dp', 'pipe')), may hold values from 0 to 31
- query_tokens: int32 [16, 32], P(('dp', 'pipe')), may hold values from 0 to 64127
- query_lengths: int32 [16], P(('dp', 'pipe')), may hold values from 1 to 32
- query_episodes: int32 [16], P(('dp', 'pipe')), may hold values from 0 to 1
- embedding: bfloat16 [64128, 4096], P(('dp', 'pipe'), 'tensor'), may hold values from -18 to 18
- attn_gain: float32 [4, 4096], P('pipe'), may hold values from 0.5 to 1.5
- query_weight: bfloat16 [4, 4096, 4096], P('pipe', None, 'tensor'), may hold values from -1 to 1
- key_weight: bfloat16 [4, 4096, 1024], P('pipe', None, 'tensor'), may hold values from -16 to 16
- value_weight: bfloat16 [4, 4096, 1024], P('pipe', None, 'tensor'), may hold values from -0.09375 to 0.09375
- out_weight: bfloat16 [4, 4096, 4096], P('pipe', 'tensor'), may hold values from -0.09375 to 0.09375
- final_gain: float32 [4096], replicated, may hold values from 0.5 to 1.5
Outputs:
- prototypes: float32 [32, 4096], P(None, 'tensor')
- logits: float32 [16, 16], P(('dp', 'pipe'))
Inputs may be any that keep to these rules, and one draw needn't show every extreme that they name: `support_labels`: every class is the label of at least one support sequence.
All inputs are finite; a program needn't handle non-finite values.
Results may differ from a plain program's by a relative error of at most 0.024.
Values may be sent and summed in bfloat16 or wider, within the bound.
No kernel may reach another device: no remote copies, remote signals or barrier semaphores. Data moves between devices by JAX's collectives and lax.ppermute only.
A program may use at most 128 MiB of HBM per device.

v0:
```python
import math
import jax
import jax.numpy as jnp
from jax import lax
from jax.sharding import PartitionSpec as P

D = 4096
HEAD_DIM = 128
WAYS = 16
EPISODES = 2
epsilon = 1e-05
rotary_base = 500000.0


def passed_along(block, axis, distance):
    devices = range(lax.axis_size(axis))
    route = [((i - distance) % len(devices), i) for i in devices]
    return lax.ppermute(block, axis, route)


def rotate(heads_in, seq_len):
    half_dim = HEAD_DIM // 2
    freqs = jnp.exp(
        -math.log(rotary_base) * jnp.arange(half_dim, dtype=jnp.float32) * (2.0 / HEAD_DIM)
    )
    angles = jnp.arange(seq_len, dtype=jnp.float32)[:, None] * freqs[None, :]
    cosine = jnp.cos(angles)[None, :, None, :]
    sine = jnp.sin(angles)[None, :, None, :]
    first_half = heads_in[..., :half_dim]
    second_half = heads_in[..., half_dim:]
    return jnp.concatenate(
        [first_half * cosine - second_half * sine, second_half * cosine + first_half * sine],
        axis=-1,
    )


def whole_rows(hidden):
    return lax.all_gather(hidden, "tensor", axis=1, tiled=True)


def whole_values(full_rows, gain_vector):
    values = full_rows.astype(jnp.float32)
    mean_square = jnp.mean(values * values, axis=-1, keepdims=True)
    return values * lax.rsqrt(mean_square + epsilon) * gain_vector


def shards(
    support_tokens,
    support_lengths,
    support_labels,
    query_tokens,
    query_lengths,
    query_episodes,
    embedding,
    attn_gain,
    query_weight,
    key_weight,
    value_weight,
    out_weight,
    final_gain,
):
    group_count = lax.axis_size(("dp", "pipe"))
    sections = lax.axis_size("pipe")
    sup_dev, seq_len = support_tokens.shape
    qry_dev = query_tokens.shape[0]
    seq_count = sup_dev + qry_dev
    row_count = seq_count * seq_len
    table_rows, width = embedding.shape
    column_start = lax.axis_index("tensor") * width
    all_support, all_query, every_sup_len, every_qry_len = (
        lax.all_gather(support_tokens, ("dp", "pipe"), axis=0, tiled=True),
        lax.all_gather(query_tokens, ("dp", "pipe"), axis=0, tiled=True),
        lax.all_gather(support_lengths, ("dp", "pipe"), axis=0, tiled=True),
        lax.all_gather(query_lengths, ("dp", "pipe"), axis=0, tiled=True),
    )
    token_flat = jnp.concatenate(
        [all_support.reshape(group_count, sup_dev * seq_len), all_query], axis=1
    ).reshape(group_count * row_count)
    local_ids = token_flat - lax.axis_index(("dp", "pipe")) * table_rows
    inside = (local_ids >= 0) & (local_ids < table_rows)
    picked = jnp.take(embedding, jnp.clip(local_ids, 0, table_rows - 1), axis=0)
    picked = jnp.where(inside[:, None], picked, jnp.zeros_like(picked))
    hidden = lax.psum_scatter(
        picked.astype(jnp.float32).astype(jnp.bfloat16),
        ("dp", "pipe"),
        scatter_dimension=0,
        tiled=True,
    )
    seq_lengths = jnp.concatenate([support_lengths, query_lengths], axis=0)
    query_proj = query_weight[0]
    key_proj = key_weight[0]
    value_proj = value_weight[0]
    out_proj = out_weight[0]
    gain_vector = attn_gain[0]
    local_heads = query_proj.shape[1] // HEAD_DIM
    local_groups = key_proj.shape[1] // HEAD_DIM
    group_size = local_heads // local_groups
    w_in = jnp.concatenate([query_proj, key_proj, value_proj], axis=1)
    query_cols = local_heads * HEAD_DIM
    key_cols = local_groups * HEAD_DIM
    positions = jnp.arange(seq_len)
    causal = positions[None, :] <= positions[:, None]

    def section_block(stream, lengths_here):
        normed = whole_values(whole_rows(stream), gain_vector).astype(jnp.bfloat16)
        projected = jnp.dot(normed, w_in, preferred_element_type=jnp.float32)
        query_heads = projected[:, :query_cols].reshape(seq_count, seq_len, local_heads, HEAD_DIM)
        key_heads = projected[:, query_cols : query_cols + key_cols].reshape(
            seq_count, seq_len, local_groups, HEAD_DIM
        )
        value_heads = (
            projected[:, query_cols + key_cols :]
            .reshape(seq_count, seq_len, local_groups, HEAD_DIM)
            .astype(jnp.bfloat16)
        )
        query_heads = (
            rotate(query_heads, seq_len)
            .astype(jnp.bfloat16)
            .reshape(seq_count, seq_len, local_groups, group_size, HEAD_DIM)
        )
        key_heads = rotate(key_heads, seq_len).astype(jnp.bfloat16)
        scores = jnp.einsum(
            "sikgd,sjkd->skgij", query_heads, key_heads, preferred_element_type=jnp.float32
        ) / math.sqrt(HEAD_DIM)
        visible = causal[None, :, :] & (positions[None, None, :] < lengths_here[:, None, None])
        scores = jnp.where(visible[:, None, None, :, :], scores, -1e30)
        weights = jax.nn.softmax(scores, axis=-1).astype(jnp.bfloat16)
        mixed = jnp.einsum(
            "skgij,sjkd->sikgd", weights, value_heads, preferred_element_type=jnp.float32
        )
        mixed = mixed.astype(jnp.bfloat16).reshape(row_count, query_cols)
        partial_out = jnp.dot(mixed, out_proj, preferred_element_type=jnp.float32)
        summed = lax.psum_scatter(
            partial_out.astype(jnp.bfloat16), "tensor", scatter_dimension=1, tiled=True
        ).astype(jnp.float32)
        return (stream.astype(jnp.float32) + summed).astype(jnp.bfloat16)

    section_index = lax.axis_index("pipe")
    dp_base = lax.axis_index("dp") * sections

    def tick(tick_index, stream):
        held_group = dp_base + (section_index - tick_index) % sections
        sup_part = lax.dynamic_slice_in_dim(every_sup_len, held_group * sup_dev, sup_dev)
        qry_part = lax.dynamic_slice_in_dim(every_qry_len, held_group * qry_dev, qry_dev)
        lengths_here = jnp.concatenate([sup_part, qry_part], axis=0)
        first_tick = (tick_index - section_index) % sections
        active = (first_tick <= tick_index) & (tick_index < first_tick + sections)
        computed = section_block(stream, lengths_here)
        stream = jnp.where(active, computed, stream)
        return passed_along(stream, "pipe", 1)

    hidden = lax.fori_loop(0, 2 * sections, tick, hidden)
    final = lax.dynamic_slice_in_dim(
        whole_values(whole_rows(hidden), final_gain), column_start, width, 1
    )
    live = (positions[None, :] < seq_lengths[:, None]).astype(jnp.float32)
    pooled = jnp.sum(
        final.reshape(seq_count, seq_len, width) * live[:, :, None], axis=1
    ) / seq_lengths[:, None].astype(jnp.float32)
    support_pooled = pooled[:sup_dev]
    query_pooled = pooled[sup_dev:]
    class_count_all = EPISODES * WAYS
    onehot = (support_labels[:, 0][:, None] == jnp.arange(class_count_all)[None, :]).astype(
        jnp.float32
    )
    class_total = jnp.dot(onehot.T, support_pooled, precision=lax.Precision.HIGHEST)
    class_count = jnp.sum(onehot, axis=0)
    class_total, class_count = (
        lax.psum(class_total.astype(jnp.bfloat16), ("dp", "pipe")).astype(jnp.float32),
        lax.psum(class_count.astype(jnp.bfloat16), ("dp", "pipe")).astype(jnp.float32),
    )
    prototypes = class_total / class_count[:, None]
    episode_pick = (query_episodes[:, None] == jnp.arange(EPISODES)[None, :]).astype(jnp.float32)
    chosen = jnp.einsum(
        "qe,ewc->qwc",
        episode_pick,
        prototypes.reshape(EPISODES, WAYS, width),
        precision=lax.Precision.HIGHEST,
    )
    partial_distance = jnp.sum((query_pooled[:, None, :] - chosen) ** 2, axis=-1)
    distance = lax.psum(partial_distance, "tensor")
    logits = -distance / math.sqrt(D)
    return (prototypes, logits)


def solution(mesh):
    return jax.shard_map(
        shards,
        mesh=mesh,
        in_specs=(
            P(("dp", "pipe"), None),
            P(("dp", "pipe")),
            P(("dp", "pipe"), None),
            P(("dp", "pipe"), None),
            P(("dp", "pipe")),
            P(("dp", "pipe")),
            P(("dp", "pipe"), "tensor"),
            P("pipe", None),
            P("pipe", None, "tensor"),
            P("pipe", None, "tensor"),
            P("pipe", None, "tensor"),
            P("pipe", "tensor", None),
            P(),
        ),
        out_specs=(P(None, "tensor"), P(("dp", "pipe"), None)),
        check_vma=False,
    )
```

profile of v0, /device:TPU:8, one launch (start us, length us, event | category | flops | bytes accessed | tf_op | source)
XLA Modules:
  0.0 830.7 jit_solution(18302538500788156600)
XLA Ops:
  7.2 29.0 %all-gather.1 = s32[16,1,32]{2,1,0:T(1,128)S(1)} all-gather(s32[1,1,32]{2,1,0:T(1,128)} %bitcast.117), channel_id=1, replica_groups=mesh['dp'=4,'pipe'=4,'tensor'=2] {'dp','pipe'}, dimensions={0}, use_global_device_ids=true | all-gather | bytes 2176 | tf_op jit(solution)/shard_map/all_gather | solution.py:72
  36.2 33.0 %all-gather = s32[16,2,32]{2,1,0:T(2,128)S(1)} all-gather(s32[1,2,32]{2,1,0:T(2,128)} %bitcast.113), channel_id=1, replica_groups=mesh['dp'=4,'pipe'=4,'tensor'=2] {'dp','pipe'}, dimensions={0}, use_global_device_ids=true | all-gather | bytes 4352 | tf_op jit(solution)/shard_map/all_gather | solution.py:71
  69.7 20.5 %gather_fusion = bf16[1536,2048]{1,0:T(8,128)(2,1)} fusion(bf16[4008,2048]{1,0:T(8,128)(2,1)} %param.21, s32[2048]{0:T(1024)S(1)} %pad_clamp_fusion), kind=kCustom, calls=%fused_computation | custom fusion | bytes 12589056 | tf_op jit(solution)/shard_map/jit(_take)/gather | solution.py:81
  108.2 18.7 %pad_maximum_fusion = bf16[4096,3072]{1,0:T(8,128)(2,1)} fusion(bf16[4096,512]{1,0:T(8,128)(2,1)} %bitcast.104, bf16[4096,512]{1,0:T(8,128)(2,1)} %bitcast.105, bf16[4096,2048]{1,0:T(8,128)(2,1)} %bitcast.99), kind=kLoop, calls=%fused_computation.54 | loop fusion | flops 75497472 | bytes 50331648 | tf_op jit(solution)/shard_map/concatenate | solution.py:98
  126.8 53.5 %reduce-scatter.3.cloned.1.call-done = bf16[96,2048]{1,0:T(8,128)(2,1)} async-done(((bf16[1536,2048]{1,0:T(8,128)(2,1)}), bf16[96,2048]{1,0:T(8,128)(2,1)}) %reduce-scatter.3.cloned.1.call-update) | async-done | bytes 393232 | tf_op jit(solution)/shard_map/reduce_scatter | solution.py:83
  180.3 532.5 %while.16 = (s32[]{:T(128)}, bf16[96,2048]{1,0:T(8,128)(2,1)}, s32[]{:T(128)}, f32[1,4096]{1,0:T(1,128)S(1)}, bf16[4096,3072]{1,0:T(8,128)(2,1)}, /*index=5*/s32...) while((s32[]{:T(128)}, bf16[96,2048]{1,0:T(8,128)(2,1)}, ...), condition=%wide.region_6.7_spmd.clone, body=%wide.region_1.0_spmd.clone.sunk | while | flops 4072005120 | bytes 66611072 | solution.py:152
  180.4 11.0 %all_gather.32 = bf16[96,4096]{1,0:T(8,128)(2,1)S(1)} all-gather(bf16[96,2048]{1,0:T(8,128)(2,1)} %get-tuple-element.408), channel_id=1, replica_groups=mesh['dp'=4,'pipe'=4,'tensor'=2] {'tensor'}, dimensions={1}, use_global_device_ids=true | all-gather | bytes 1179648 | tf_op jit(solution)/shard_map/while/body/eval_jaxpr/all_gather | solution.py:38
  191.6 10.4 %fusion.89 = f32[96,3072]{1,0:T(8,128)S(1)} fusion(bf16[4096,3072]{1,0:T(8,128)(2,1)} %get-tuple-element.427, bf16[96,4096]{1,0:T(8,128)(2,1)S(1)} %all_gather.32, f32[4096]{0:T(1024)S(1)} %bitcast.108, f32[96]{0:T(128)S(1)} %add_rsqrt_fusion.3), kind=kOutput, calls=%fused_computation.17.clone.1 | convolution fusion | flops 2417491968 | bytes 27148672 | tf_op jit(solution)/shard_map/while/body/eval_jaxpr/dot_general | solution.py:106
  207.3 9.5 %convolution_convert_fusion.4 = bf16[96,4096]{1,0:T(8,128)(2,1)} fusion(bf16[96,2048]{1,0:T(8,128)(2,1)S(1)} %reshape.325, bf16[2048,4096]{1,0:T(8,128)(2,1)} %get-tuple-element.431), kind=kOutput, calls=%fused_computation.4.clone.1 | convolution fusion | flops 1611005952 | bytes 17956864 | tf_op jit(solution)/shard_map/while/body/eval_jaxpr/dot_general | solution.py:132
  216.9 17.6 %reduce-scatter.5.cloned.1.call-done = bf16[96,2048]{1,0:T(8,128)(2,1)} async-done(((bf16[96,4096]{1,0:T(8,128)(2,1)}), bf16[96,2048]{1,0:T(8,128)(2,1)}) %reduce-scatter.5.cloned.1.call-update) | async-done | bytes 393232 | tf_op jit(solution)/shard_map/while/body/eval_jaxpr/reduce_scatter | solution.py:133
  237.1 9.2 %collective-permute-done = bf16[96,2048]{1,0:T(8,128)(2,1)S(1)} collective-permute-done((bf16[96,2048]{1,0:T(8,128)(2,1)S(1)}, bf16[96,2048]{1,0:T(8,128)(2,1)S(1)}, u32[]{:S(2)}, u32[]{:S(2)}) %collective-permute-start) | collective-permute-done | bytes 393248 | tf_op jit(solution)/shard_map/while/body/eval_jaxpr/ppermute | solution.py:18
  247.2 10.7 %all_gather.32 = bf16[96,4096]{1,0:T(8,128)(2,1)S(1)} all-gather(bf16[96,2048]{1,0:T(8,128)(2,1)} %get-tuple-element.408), channel_id=1, replica_groups=mesh['dp'=4,'pipe'=4,'tensor'=2] {'tensor'}, dimensions={1}, use_global_device_ids=true | all-gather | bytes 1179648 | tf_op jit(solution)/shard_map/while/body/eval_jaxpr/all_gather | solution.py:38
  258.1 10.4 %fusion.89 = f32[96,3072]{1,0:T(8,128)S(1)} fusion(bf16[4096,3072]{1,0:T(8,128)(2,1)} %get-tuple-element.427, bf16[96,4096]{1,0:T(8,128)(2,1)S(1)} %all_gather.32, f32[4096]{0:T(1024)S(1)} %bitcast.108, f32[96]{0:T(128)S(1)} %add_rsqrt_fusion.3), kind=kOutput, calls=%fused_computation.17.clone.1 | convolution fusion | flops 2417491968 | bytes 27148672 | tf_op jit(solution)/shard_map/while/body/eval_jaxpr/dot_general | solution.py:106
  273.8 9.5 %convolution_convert_fusion.4 = bf16[96,4096]{1,0:T(8,128)(2,1)} fusion(bf16[96,2048]{1,0:T(8,128)(2,1)S(1)} %reshape.325, bf16[2048,4096]{1,0:T(8,128)(2,1)} %get-tuple-element.431), kind=kOutput, calls=%fused_computation.4.clone.1 | convolution fusion | flops 1611005952 | bytes 17956864 | tf_op jit(solution)/shard_map/while/body/eval_jaxpr/dot_general | solution.py:132
  283.4 17.6 %reduce-scatter.5.cloned.1.call-done = bf16[96,2048]{1,0:T(8,128)(2,1)} async-done(((bf16[96,4096]{1,0:T(8,128)(2,1)}), bf16[96,2048]{1,0:T(8,128)(2,1)}) %reduce-scatter.5.cloned.1.call-update) | async-done | bytes 393232 | tf_op jit(solution)/shard_map/while/body/eval_jaxpr/reduce_scatter | solution.py:133
  303.7 9.2 %collective-permute-done = bf16[96,2048]{1,0:T(8,128)(2,1)S(1)} collective-permute-done((bf16[96,2048]{1,0:T(8,128)(2,1)S(1)}, bf16[96,2048]{1,0:T(8,128)(2,1)S(1)}, u32[]{:S(2)}, u32[]{:S(2)}) %collective-permute-start) | collective-permute-done | bytes 393248 | tf_op jit(solution)/shard_map/while/body/eval_jaxpr/ppermute | solution.py:18
  313.7 10.7 %all_gather.32 = bf16[96,4096]{1,0:T(8,128)(2,1)S(1)} all-gather(bf16[96,2048]{1,0:T(8,128)(2,1)} %get-tuple-element.408), channel_id=1, replica_groups=mesh['dp'=4,'pipe'=4,'tensor'=2] {'tensor'}, dimensions={1}, use_global_device_ids=true | all-gather | bytes 1179648 | tf_op jit(solution)/shard_map/while/body/eval_jaxpr/all_gather | solution.py:38
  324.6 10.4 %fusion.89 = f32[96,3072]{1,0:T(8,128)S(1)} fusion(bf16[4096,3072]{1,0:T(8,128)(2,1)} %get-tuple-element.427, bf16[96,4096]{1,0:T(8,128)(2,1)S(1)} %all_gather.32, f32[4096]{0:T(1024)S(1)} %bitcast.108, f32[96]{0:T(128)S(1)} %add_rsqrt_fusion.3), kind=kOutput, calls=%fused_computation.17.clone.1 | convolution fusion | flops 2417491968 | bytes 27148672 | tf_op jit(solution)/shard_map/while/body/eval_jaxpr/dot_general | solution.py:106
  340.3 9.5 %convolution_convert_fusion.4 = bf16[96,4096]{1,0:T(8,128)(2,1)} fusion(bf16[96,2048]{1,0:T(8,128)(2,1)S(1)} %reshape.325, bf16[2048,4096]{1,0:T(8,128)(2,1)} %get-tuple-element.431), kind=kOutput, calls=%fused_computation.4.clone.1 | convolution fusion | flops 1611005952 | bytes 17956864 | tf_op jit(solution)/shard_map/while/body/eval_jaxpr/dot_general | solution.py:132
  349.9 17.7 %reduce-scatter.5.cloned.1.call-done = bf16[96,2048]{1,0:T(8,128)(2,1)} async-done(((bf16[96,4096]{1,0:T(8,128)(2,1)}), bf16[96,2048]{1,0:T(8,128)(2,1)}) %reduce-scatter.5.cloned.1.call-update) | async-done | bytes 393232 | tf_op jit(solution)/shard_map/while/body/eval_jaxpr/reduce_scatter | solution.py:133
  380.2 10.7 %all_gather.32 = bf16[96,4096]{1,0:T(8,128)(2,1)S(1)} all-gather(bf16[96,2048]{1,0:T(8,128)(2,1)} %get-tuple-element.408), channel_id=1, replica_groups=mesh['dp'=4,'pipe'=4,'tensor'=2] {'tensor'}, dimensions={1}, use_global_device_ids=true | all-gather | bytes 1179648 | tf_op jit(solution)/shard_map/while/body/eval_jaxpr/all_gather | solution.py:38
  391.2 10.4 %fusion.89 = f32[96,3072]{1,0:T(8,128)S(1)} fusion(bf16[4096,3072]{1,0:T(8,128)(2,1)} %get-tuple-element.427, bf16[96,4096]{1,0:T(8,128)(2,1)S(1)} %all_gather.32, f32[4096]{0:T(1024)S(1)} %bitcast.108, f32[96]{0:T(128)S(1)} %add_rsqrt_fusion.3), kind=kOutput, calls=%fused_computation.17.clone.1 | convolution fusion | flops 2417491968 | bytes 27148672 | tf_op jit(solution)/shard_map/while/body/eval_jaxpr/dot_general | solution.py:106
  406.8 9.5 %convolution_convert_fusion.4 = bf16[96,4096]{1,0:T(8,128)(2,1)} fusion(bf16[96,2048]{1,0:T(8,128)(2,1)S(1)} %reshape.325, bf16[2048,4096]{1,0:T(8,128)(2,1)} %get-tuple-element.431), kind=kOutput, calls=%fused_computation.4.clone.1 | convolution fusion | flops 1611005952 | bytes 17956864 | tf_op jit(solution)/shard_map/while/body/eval_jaxpr/dot_general | solution.py:132
  416.4 17.6 %reduce-scatter.5.cloned.1.call-done = bf16[96,2048]{1,0:T(8,128)(2,1)} async-done(((bf16[96,4096]{1,0:T(8,128)(2,1)}), bf16[96,2048]{1,0:T(8,128)(2,1)}) %reduce-scatter.5.cloned.1.call-update) | async-done | bytes 393232 | tf_op jit(solution)/shard_map/while/body/eval_jaxpr/reduce_scatter | solution.py:133
  436.7 9.2 %collective-permute-done = bf16[96,2048]{1,0:T(8,128)(2,1)S(1)} collective-permute-done((bf16[96,2048]{1,0:T(8,128)(2,1)S(1)}, bf16[96,2048]{1,0:T(8,128)(2,1)S(1)}, u32[]{:S(2)}, u32[]{:S(2)}) %collective-permute-start) | collective-permute-done | bytes 393248 | tf_op jit(solution)/shard_map/while/body/eval_jaxpr/ppermute | solution.py:18
  446.7 10.7 %all_gather.32 = bf16[96,4096]{1,0:T(8,128)(2,1)S(1)} all-gather(bf16[96,2048]{1,0:T(8,128)(2,1)} %get-tuple-element.408), channel_id=1, replica_groups=mesh['dp'=4,'pipe'=4,'tensor'=2] {'tensor'}, dimensions={1}, use_global_device_ids=true | all-gather | bytes 1179648 | tf_op jit(solution)/shard_map/while/body/eval_jaxpr/all_gather | solution.py:38
  457.7 10.4 %fusion.89 = f32[96,3072]{1,0:T(8,128)S(1)} fusion(bf16[4096,3072]{1,0:T(8,128)(2,1)} %get-tuple-element.427, bf16[96,4096]{1,0:T(8,128)(2,1)S(1)} %all_gather.32, f32[4096]{0:T(1024)S(1)} %bitcast.108, f32[96]{0:T(128)S(1)} %add_rsqrt_fusion.3), kind=kOutput, calls=%fused_computation.17.clone.1 | convolution fusion | flops 2417491968 | bytes 27148672 | tf_op jit(solution)/shard_map/while/body/eval_jaxpr/dot_general | solution.py:106
  473.4 9.5 %convolution_convert_fusion.4 = bf16[96,4096]{1,0:T(8,128)(2,1)} fusion(bf16[96,2048]{1,0:T(8,128)(2,1)S(1)} %reshape.325, bf16[2048,4096]{1,0:T(8,128)(2,1)} %get-tuple-element.431), kind=kOutput, calls=%fused_computation.4.clone.1 | convolution fusion | flops 1611005952 | bytes 17956864 | tf_op jit(solution)/shard_map/while/body/eval_jaxpr/dot_general | solution.py:132
  483.0 17.6 %reduce-scatter.5.cloned.1.call-done = bf16[96,2048]{1,0:T(8,128)(2,1)} async-done(((bf16[96,4096]{1,0:T(8,128)(2,1)}), bf16[96,2048]{1,0:T(8,128)(2,1)}) %reduce-scatter.5.cloned.1.call-update) | async-done | bytes 393232 | tf_op jit(solution)/shard_map/while/body/eval_jaxpr/reduce_scatter | solution.py:133
  503.3 9.2 %collective-permute-done = bf16[96,2048]{1,0:T(8,128)(2,1)S(1)} collective-permute-done((bf16[96,2048]{1,0:T(8,128)(2,1)S(1)}, bf16[96,2048]{1,0:T(8,128)(2,1)S(1)}, u32[]{:S(2)}, u32[]{:S(2)}) %collective-permute-start) | collective-permute-done | bytes 393248 | tf_op jit(solution)/shard_map/while/body/eval_jaxpr/ppermute | solution.py:18
  513.3 10.7 %all_gather.32 = bf16[96,4096]{1,0:T(8,128)(2,1)S(1)} all-gather(bf16[96,2048]{1,0:T(8,128)(2,1)} %get-tuple-element.408), channel_id=1, replica_groups=mesh['dp'=4,'pipe'=4,'tensor'=2] {'tensor'}, dimensions={1}, use_global_device_ids=true | all-gather | bytes 1179648 | tf_op jit(solution)/shard_map/while/body/eval_jaxpr/all_gather | solution.py:38
  524.2 10.4 %fusion.89 = f32[96,3072]{1,0:T(8,128)S(1)} fusion(bf16[4096,3072]{1,0:T(8,128)(2,1)} %get-tuple-element.427, bf16[96,4096]{1,0:T(8,128)(2,1)S(1)} %all_gather.32, f32[4096]{0:T(1024)S(1)} %bitcast.108, f32[96]{0:T(128)S(1)} %add_rsqrt_fusion.3), kind=kOutput, calls=%fused_computation.17.clone.1 | convolution fusion | flops 2417491968 | bytes 27148672 | tf_op jit(solution)/shard_map/while/body/eval_jaxpr/dot_general | solution.py:106
  539.9 9.5 %convolution_convert_fusion.4 = bf16[96,4096]{1,0:T(8,128)(2,1)} fusion(bf16[96,2048]{1,0:T(8,128)(2,1)S(1)} %reshape.325, bf16[2048,4096]{1,0:T(8,128)(2,1)} %get-tuple-element.431), kind=kOutput, calls=%fused_computation.4.clone.1 | convolution fusion | flops 1611005952 | bytes 17956864 | tf_op jit(solution)/shard_map/while/body/eval_jaxpr/dot_general | solution.py:132
  549.5 17.6 %reduce-scatter.5.cloned.1.call-done = bf16[96,2048]{1,0:T(8,128)(2,1)} async-done(((bf16[96,4096]{1,0:T(8,128)(2,1)}), bf16[96,2048]{1,0:T(8,128)(2,1)}) %reduce-scatter.5.cloned.1.call-update) | async-done | bytes 393232 | tf_op jit(solution)/shard_map/while/body/eval_jaxpr/reduce_scatter | solution.py:133
  569.8 9.2 %collective-permute-done = bf16[96,2048]{1,0:T(8,128)(2,1)S(1)} collective-permute-done((bf16[96,2048]{1,0:T(8,128)(2,1)S(1)}, bf16[96,2048]{1,0:T(8,128)(2,1)S(1)}, u32[]{:S(2)}, u32[]{:S(2)}) %collective-permute-start) | collective-permute-done | bytes 393248 | tf_op jit(solution)/shard_map/while/body/eval_jaxpr/ppermute | solution.py:18
  579.8 10.7 %all_gather.32 = bf16[96,4096]{1,0:T(8,128)(2,1)S(1)} all-gather(bf16[96,2048]{1,0:T(8,128)(2,1)} %get-tuple-element.408), channel_id=1, replica_groups=mesh['dp'=4,'pipe'=4,'tensor'=2] {'tensor'}, dimensions={1}, use_global_device_ids=true | all-gather | bytes 1179648 | tf_op jit(solution)/shard_map/while/body/eval_jaxpr/all_gather | solution.py:38
  590.8 10.4 %fusion.89 = f32[96,3072]{1,0:T(8,128)S(1)} fusion(bf16[4096,3072]{1,0:T(8,128)(2,1)} %get-tuple-element.427, bf16[96,4096]{1,0:T(8,128)(2,1)S(1)} %all_gather.32, f32[4096]{0:T(1024)S(1)} %bitcast.108, f32[96]{0:T(128)S(1)} %add_rsqrt_fusion.3), kind=kOutput, calls=%fused_computation.17.clone.1 | convolution fusion | flops 2417491968 | bytes 27148672 | tf_op jit(solution)/shard_map/while/body/eval_jaxpr/dot_general | solution.py:106
  606.5 9.5 %convolution_convert_fusion.4 = bf16[96,4096]{1,0:T(8,128)(2,1)} fusion(bf16[96,2048]{1,0:T(8,128)(2,1)S(1)} %reshape.325, bf16[2048,4096]{1,0:T(8,128)(2,1)} %get-tuple-element.431), kind=kOutput, calls=%fused_computation.4.clone.1 | convolution fusion | flops 1611005952 | bytes 17956864 | tf_op jit(solution)/shard_map/while/body/eval_jaxpr/dot_general | solution.py:132
  616.0 17.6 %reduce-scatter.5.cloned.1.call-done = bf16[96,2048]{1,0:T(8,128)(2,1)} async-done(((bf16[96,4096]{1,0:T(8,128)(2,1)}), bf16[96,2048]{1,0:T(8,128)(2,1)}) %reduce-scatter.5.cloned.1.call-update) | async-done | bytes 393232 | tf_op jit(solution)/shard_map/while/body/eval_jaxpr/reduce_scatter | solution.py:133
  636.3 9.2 %collective-permute-done = bf16[96,2048]{1,0:T(8,128)(2,1)S(1)} collective-permute-done((bf16[96,2048]{1,0:T(8,128)(2,1)S(1)}, bf16[96,2048]{1,0:T(8,128)(2,1)S(1)}, u32[]{:S(2)}, u32[]{:S(2)}) %collective-permute-start) | collective-permute-done | bytes 393248 | tf_op jit(solution)/shard_map/while/body/eval_jaxpr/ppermute | solution.py:18
  646.3 10.7 %all_gather.32 = bf16[96,4096]{1,0:T(8,128)(2,1)S(1)} all-gather(bf16[96,2048]{1,0:T(8,128)(2,1)} %get-tuple-element.408), channel_id=1, replica_groups=mesh['dp'=4,'pipe'=4,'tensor'=2] {'tensor'}, dimensions={1}, use_global_device_ids=true | all-gather | bytes 1179648 | tf_op jit(solution)/shard_map/while/body/eval_jaxpr/all_gather | solution.py:38
  657.3 10.4 %fusion.89 = f32[96,3072]{1,0:T(8,128)S(1)} fusion(bf16[4096,3072]{1,0:T(8,128)(2,1)} %get-tuple-element.427, bf16[96,4096]{1,0:T(8,128)(2,1)S(1)} %all_gather.32, f32[4096]{0:T(1024)S(1)} %bitcast.108, f32[96]{0:T(128)S(1)} %add_rsqrt_fusion.3), kind=kOutput, calls=%fused_computation.17.clone.1 | convolution fusion | flops 2417491968 | bytes 27148672 | tf_op jit(solution)/shard_map/while/body/eval_jaxpr/dot_general | solution.py:106
  673.0 9.5 %convolution_convert_fusion.4 = bf16[96,4096]{1,0:T(8,128)(2,1)} fusion(bf16[96,2048]{1,0:T(8,128)(2,1)S(1)} %reshape.325, bf16[2048,4096]{1,0:T(8,128)(2,1)} %get-tuple-element.431), kind=kOutput, calls=%fused_computation.4.clone.1 | convolution fusion | flops 1611005952 | bytes 17956864 | tf_op jit(solution)/shard_map/while/body/eval_jaxpr/dot_general | solution.py:132
  682.5 17.6 %reduce-scatter.5.cloned.1.call-done = bf16[96,2048]{1,0:T(8,128)(2,1)} async-done(((bf16[96,4096]{1,0:T(8,128)(2,1)}), bf16[96,2048]{1,0:T(8,128)(2,1)}) %reduce-scatter.5.cloned.1.call-update) | async-done | bytes 393232 | tf_op jit(solution)/shard_map/while/body/eval_jaxpr/reduce_scatter | solution.py:133
  702.8 9.2 %collective-permute-done = bf16[96,2048]{1,0:T(8,128)(2,1)S(1)} collective-permute-done((bf16[96,2048]{1,0:T(8,128)(2,1)S(1)}, bf16[96,2048]{1,0:T(8,128)(2,1)S(1)}, u32[]{:S(2)}, u32[]{:S(2)}) %collective-permute-start) | collective-permute-done | bytes 393248 | tf_op jit(solution)/shard_map/while/body/eval_jaxpr/ppermute | solution.py:18
  712.8 10.8 %all_gather.29 = bf16[96,4096]{1,0:T(8,128)(2,1)S(1)} all-gather(bf16[96,2048]{1,0:T(8,128)(2,1)} %get-tuple-element.268), channel_id=1, replica_groups=mesh['dp'=4,'pipe'=4,'tensor'=2] {'tensor'}, dimensions={1}, use_global_device_ids=true | all-gather | bytes 1179648 | tf_op jit(solution)/shard_map/all_gather | solution.py:38
  725.6 32.3 %psum.22 = bf16[32]{0:T(256)(128)(2,1)S(1)} all-reduce(bf16[32]{0:T(256)(128)(2,1)S(1)} %convert_reduce_fusion), channel_id=1, replica_groups=mesh['dp'=4,'pipe'=4,'tensor'=2] {'dp','pipe'}, use_global_device_ids=true, to_apply=%region_11.12 | all-reduce | flops 32 | bytes 128 | tf_op jit(solution)/shard_map/psum | solution.py:170
  758.6 57.9 %all-reduce.5.cloned.1.call-done = bf16[32,2048]{1,0:T(8,128)(2,1)} async-done(((bf16[32,2048]{1,0:T(8,128)(2,1)}), bf16[32,2048]{1,0:T(8,128)(2,1)}) %all-reduce.5.cloned.1.call-update) | async-done | bytes 131088 | tf_op jit(solution)/shard_map/psum | solution.py:169
  (314 shorter events, 106.5 us)
Async XLA Ops:
  7.2 173.2 %reduce-scatter.3.cloned.1.call-start = ((), (), s32[]{:S(2)}) async-start(), calls=%async_computation.2 | async-start | bytes 6684672 | tf_op jit(solution)/shard_map/reduce_scatter | solution.py:83
  97.3 0.7 copy-start.6
  97.3 2.1 copy-start.5
  108.2 72.1 %copy-start.2 = (f32[1,4096]{1,0:T(1,128)S(1)}, f32[1,4096]{1,0:T(1,128)}, u32[]{:S(2)}) copy-start(f32[1,4096]{1,0:T(1,128)} %param.22) | copy-start | bytes 49156
  180.3 543.7 %dynamic-slice-start = ((f32[4096]{0:T(1024)}, s32[]{:T(128)}), f32[2048]{0:T(1024)S(1)}, s32[]{:S(2)}) async-start(f32[4096]{0:T(1024)} %param.27, s32[]{:T(128)} %select_n.115), calls=%async_computation.5 | async-start | bytes 16896 | tf_op jit(solution)/shard_map/dynamic_slice | solution.py:153
  180.3 54.2 %reduce-scatter.5.cloned.1.call-start = ((), (), s32[]{:S(2)}) async-start(), calls=%async_computation.4 | async-start | bytes 1179648 | tf_op jit(solution)/shard_map/while/body/eval_jaxpr/reduce_scatter | solution.py:133
  207.3 27.2 %copy-start = (bf16[96,2048]{1,0:T(8,128)(2,1)S(1)}, bf16[96,2048]{1,0:T(8,128)(2,1)}, u32[]{:S(2)}) copy-start(bf16[96,2048]{1,0:T(8,128)(2,1)} %get-tuple-element.408) | copy-start | bytes 1179652 | tf_op jit(solution)/shard_map/while
  235.6 10.8 %collective-permute-start = (bf16[96,2048]{1,0:T(8,128)(2,1)S(1)}, bf16[96,2048]{1,0:T(8,128)(2,1)S(1)}, u32[]{:S(2)}, u32[]{:S(2)}) collective-permute-start(bf16[96,2048]{1,0:T(8,128)(2,1)S(1)} %fusion.94), channel_id=1, source_target_pairs={{6,0},{0,2},{2,4},{4,6},{7,1},{1,3},{3,5},{5,7},{14,8},{8,10},{10,... | collective-permute-start | bytes 1179656 | tf_op jit(solution)/shard_map/while/body/eval_jaxpr/ppermute | solution.py:18
  246.4 0.8 copy-start.1
  247.1 53.9 %reduce-scatter.5.cloned.1.call-start = ((), (), s32[]{:S(2)}) async-start(), calls=%async_computation.4 | async-start | bytes 1179648 | tf_op jit(solution)/shard_map/while/body/eval_jaxpr/reduce_scatter | solution.py:133
  273.8 27.2 %copy-start = (bf16[96,2048]{1,0:T(8,128)(2,1)S(1)}, bf16[96,2048]{1,0:T(8,128)(2,1)}, u32[]{:S(2)}) copy-start(bf16[96,2048]{1,0:T(8,128)(2,1)} %get-tuple-element.408) | copy-start | bytes 1179652 | tf_op jit(solution)/shard_map/while
  302.1 10.7 %collective-permute-start = (bf16[96,2048]{1,0:T(8,128)(2,1)S(1)}, bf16[96,2048]{1,0:T(8,128)(2,1)S(1)}, u32[]{:S(2)}, u32[]{:S(2)}) collective-permute-start(bf16[96,2048]{1,0:T(8,128)(2,1)S(1)} %fusion.94), channel_id=1, source_target_pairs={{6,0},{0,2},{2,4},{4,6},{7,1},{1,3},{3,5},{5,7},{14,8},{8,10},{10,... | collective-permute-start | bytes 1179656 | tf_op jit(solution)/shard_map/while/body/eval_jaxpr/ppermute | solution.py:18
  312.9 0.8 copy-start.1
  313.6 53.9 %reduce-scatter.5.cloned.1.call-start = ((), (), s32[]{:S(2)}) async-start(), calls=%async_computation.4 | async-start | bytes 1179648 | tf_op jit(solution)/shard_map/while/body/eval_jaxpr/reduce_scatter | solution.py:133
  340.3 27.3 %copy-start = (bf16[96,2048]{1,0:T(8,128)(2,1)S(1)}, bf16[96,2048]{1,0:T(8,128)(2,1)}, u32[]{:S(2)}) copy-start(bf16[96,2048]{1,0:T(8,128)(2,1)} %get-tuple-element.408) | copy-start | bytes 1179652 | tf_op jit(solution)/shard_map/while
  368.7 10.7 %collective-permute-start = (bf16[96,2048]{1,0:T(8,128)(2,1)S(1)}, bf16[96,2048]{1,0:T(8,128)(2,1)S(1)}, u32[]{:S(2)}, u32[]{:S(2)}) collective-permute-start(bf16[96,2048]{1,0:T(8,128)(2,1)S(1)} %fusion.94), channel_id=1, source_target_pairs={{6,0},{0,2},{2,4},{4,6},{7,1},{1,3},{3,5},{5,7},{14,8},{8,10},{10,... | collective-permute-start | bytes 1179656 | tf_op jit(solution)/shard_map/while/body/eval_jaxpr/ppermute | solution.py:18
  379.4 0.8 copy-start.1
  380.2 53.9 %reduce-scatter.5.cloned.1.call-start = ((), (), s32[]{:S(2)}) async-start(), calls=%async_computation.4 | async-start | bytes 1179648 | tf_op jit(solution)/shard_map/while/body/eval_jaxpr/reduce_scatter | solution.py:133
  406.8 27.2 %copy-start = (bf16[96,2048]{1,0:T(8,128)(2,1)S(1)}, bf16[96,2048]{1,0:T(8,128)(2,1)}, u32[]{:S(2)}) copy-start(bf16[96,2048]{1,0:T(8,128)(2,1)} %get-tuple-element.408) | copy-start | bytes 1179652 | tf_op jit(solution)/shard_map/while
  435.2 10.8 %collective-permute-start = (bf16[96,2048]{1,0:T(8,128)(2,1)S(1)}, bf16[96,2048]{1,0:T(8,128)(2,1)S(1)}, u32[]{:S(2)}, u32[]{:S(2)}) collective-permute-start(bf16[96,2048]{1,0:T(8,128)(2,1)S(1)} %fusion.94), channel_id=1, source_target_pairs={{6,0},{0,2},{2,4},{4,6},{7,1},{1,3},{3,5},{5,7},{14,8},{8,10},{10,... | collective-permute-start | bytes 1179656 | tf_op jit(solution)/shard_map/while/body/eval_jaxpr/ppermute | solution.py:18
  445.9 0.8 copy-start.1
  446.7 53.9 %reduce-scatter.5.cloned.1.call-start = ((), (), s32[]{:S(2)}) async-start(), calls=%async_computation.4 | async-start | bytes 1179648 | tf_op jit(solution)/shard_map/while/body/eval_jaxpr/reduce_scatter | solution.py:133
  473.4 27.2 %copy-start = (bf16[96,2048]{1,0:T(8,128)(2,1)S(1)}, bf16[96,2048]{1,0:T(8,128)(2,1)}, u32[]{:S(2)}) copy-start(bf16[96,2048]{1,0:T(8,128)(2,1)} %get-tuple-element.408) | copy-start | bytes 1179652 | tf_op jit(solution)/shard_map/while
  501.7 10.7 %collective-permute-start = (bf16[96,2048]{1,0:T(8,128)(2,1)S(1)}, bf16[96,2048]{1,0:T(8,128)(2,1)S(1)}, u32[]{:S(2)}, u32[]{:S(2)}) collective-permute-start(bf16[96,2048]{1,0:T(8,128)(2,1)S(1)} %fusion.94), channel_id=1, source_target_pairs={{6,0},{0,2},{2,4},{4,6},{7,1},{1,3},{3,5},{5,7},{14,8},{8,10},{10,... | collective-permute-start | bytes 1179656 | tf_op jit(solution)/shard_map/while/body/eval_jaxpr/ppermute | solution.py:18
  512.5 0.8 copy-start.1
  513.2 53.9 %reduce-scatter.5.cloned.1.call-start = ((), (), s32[]{:S(2)}) async-start(), calls=%async_computation.4 | async-start | bytes 1179648 | tf_op jit(solution)/shard_map/while/body/eval_jaxpr/reduce_scatter | solution.py:133
  539.9 27.2 %copy-start = (bf16[96,2048]{1,0:T(8,128)(2,1)S(1)}, bf16[96,2048]{1,0:T(8,128)(2,1)}, u32[]{:S(2)}) copy-start(bf16[96,2048]{1,0:T(8,128)(2,1)} %get-tuple-element.408) | copy-start | bytes 1179652 | tf_op jit(solution)/shard_map/while
  568.2 10.8 %collective-permute-start = (bf16[96,2048]{1,0:T(8,128)(2,1)S(1)}, bf16[96,2048]{1,0:T(8,128)(2,1)S(1)}, u32[]{:S(2)}, u32[]{:S(2)}) collective-permute-start(bf16[96,2048]{1,0:T(8,128)(2,1)S(1)} %fusion.94), channel_id=1, source_target_pairs={{6,0},{0,2},{2,4},{4,6},{7,1},{1,3},{3,5},{5,7},{14,8},{8,10},{10,... | collective-permute-start | bytes 1179656 | tf_op jit(solution)/shard_map/while/body/eval_jaxpr/ppermute | solution.py:18
  579.0 0.8 copy-start.1
  579.8 53.8 %reduce-scatter.5.cloned.1.call-start = ((), (), s32[]{:S(2)}) async-start(), calls=%async_computation.4 | async-start | bytes 1179648 | tf_op jit(solution)/shard_map/while/body/eval_jaxpr/reduce_scatter | solution.py:133
  606.5 27.2 %copy-start = (bf16[96,2048]{1,0:T(8,128)(2,1)S(1)}, bf16[96,2048]{1,0:T(8,128)(2,1)}, u32[]{:S(2)}) copy-start(bf16[96,2048]{1,0:T(8,128)(2,1)} %get-tuple-element.408) | copy-start | bytes 1179652 | tf_op jit(solution)/shard_map/while
  634.8 10.8 %collective-permute-start = (bf16[96,2048]{1,0:T(8,128)(2,1)S(1)}, bf16[96,2048]{1,0:T(8,128)(2,1)S(1)}, u32[]{:S(2)}, u32[]{:S(2)}) collective-permute-start(bf16[96,2048]{1,0:T(8,128)(2,1)S(1)} %fusion.94), channel_id=1, source_target_pairs={{6,0},{0,2},{2,4},{4,6},{7,1},{1,3},{3,5},{5,7},{14,8},{8,10},{10,... | collective-permute-start | bytes 1179656 | tf_op jit(solution)/shard_map/while/body/eval_jaxpr/ppermute | solution.py:18
  645.5 0.8 copy-start.1
  646.3 53.9 %reduce-scatter.5.cloned.1.call-start = ((), (), s32[]{:S(2)}) async-start(), calls=%async_computation.4 | async-start | bytes 1179648 | tf_op jit(solution)/shard_map/while/body/eval_jaxpr/reduce_scatter | solution.py:133
  673.0 27.2 %copy-start = (bf16[96,2048]{1,0:T(8,128)(2,1)S(1)}, bf16[96,2048]{1,0:T(8,128)(2,1)}, u32[]{:S(2)}) copy-start(bf16[96,2048]{1,0:T(8,128)(2,1)} %get-tuple-element.408) | copy-start | bytes 1179652 | tf_op jit(solution)/shard_map/while
  701.3 10.7 %collective-permute-start = (bf16[96,2048]{1,0:T(8,128)(2,1)S(1)}, bf16[96,2048]{1,0:T(8,128)(2,1)S(1)}, u32[]{:S(2)}, u32[]{:S(2)}) collective-permute-start(bf16[96,2048]{1,0:T(8,128)(2,1)S(1)} %fusion.94), channel_id=1, source_target_pairs={{6,0},{0,2},{2,4},{4,6},{7,1},{1,3},{3,5},{5,7},{14,8},{8,10},{10,... | collective-permute-start | bytes 1179656 | tf_op jit(solution)/shard_map/while/body/eval_jaxpr/ppermute | solution.py:18
  712.0 0.8 copy-start.1
  712.8 11.6 %copy-start.4 = (s32[2,1]{0,1:T(1,128)S(1)}, s32[2,1]{0,1:T(1,128)}, u32[]{:S(2)}) copy-start(s32[2,1]{0,1:T(1,128)} %param.17) | copy-start | bytes 28
  712.8 103.8 %all-reduce.5.cloned.1.call-start = ((), (), s32[]{:S(2)}) async-start(), calls=%async_computation.3 | async-start | bytes 262144 | tf_op jit(solution)/shard_map/psum | solution.py:169
  817.6 6.3 copy-start.3
Sparse Core Ops, SparseCore 0:
  97.4 82.8 reduce-scatter.2
  217.0 17.4 reduce-scatter.4
  283.5 17.4 reduce-scatter.4
  350.0 17.5 reduce-scatter.4
  416.5 17.4 reduce-scatter.4
  483.1 17.5 reduce-scatter.4
  549.6 17.4 reduce-scatter.4
  616.1 17.4 reduce-scatter.4
  682.6 17.4 reduce-scatter.4
  725.7 90.8 all-reduce.4
where the time goes:
time: 832 us; the launch traced here: 831 us
  waiting for transfers between devices  326 us (39%)
  blocking collectives  204 us (25%)
  matrix products  177 us (21%)
  other arithmetic  50.2 us (6%)
  local copies, waits for them, and re-layouts  43.8 us (5%)
  between operations  16.2 us (2%)
  starting transfers between devices  12.4 us (1%)
    reduce_scatter x8, waiting for transfers between devices, section_block(): lax.psum_scatter(partial_out.astype(jnp.bfloat16), 'tensor', scatter_dime...  141 us
    all_gather x9, blocking collectives, whole_rows(): return lax.all_gather(hidden, 'tensor', axis=1, tiled=True)  96.8 us
    dot_general x8, matrix products, section_block(): projected = jnp.dot(normed, w_in, preferred_element_type=jnp.float32)  83.3 us
    dot_general x8, matrix products, section_block(): partial_out = jnp.dot(mixed, out_proj, preferred_element_type=jnp.float32)  76.2 us
    ppermute x8, waiting for transfers between devices, passed_along(): return lax.ppermute(block, axis, route)  73.6 us
    psum x1, waiting for transfers between devices, shards(): lax.psum(class_total.astype(jnp.bfloat16), ('dp', 'pipe'))  57.9 us
    reduce_scatter x1, waiting for transfers between devices, shards(): lax.psum_scatter(picked.astype(jnp.float32).astype(jnp.bfloat16), ('dp',...  53.5 us
    all_gather x1, blocking collectives, shards(): lax.all_gather(support_tokens, ('dp', 'pipe'), axis=0, tiled=True)  33 us
  transfers between devices with their start and end apart: 18, of which 18 were waited for; matrix products, arithmetic and copies ran while one was open for 2% of the time, Pallas kernels for 0%

commit v1 on v0

--- a/solution.py
+++ b/solution.py
@@ -35,7 +35,9 @@
 
 
 def whole_rows(hidden):
-    return lax.all_gather(hidden, "tensor", axis=1, tiled=True)
+    return jnp.concatenate(
+        lax.all_to_all(jnp.stack([hidden] * lax.axis_size("tensor")), "tensor", 0, 0), axis=1
+    )
 
 
 def whole_values(full_rows, gain_vector):

time: 832 us -> 865 us (1.040)
  blocking collectives: 204 us -> 107 us
  waiting for transfers between devices: 326 us -> 402 us
  starting transfers between devices: 12.4 us -> 44.4 us
  other arithmetic: 50.2 us -> 70.5 us
    all_gather x9 -> x0, blocking collectives: 96.8 us -> none  [whole_rows(): return lax.all_gather(hidden, 'tensor', axis=1, tiled=True)]
    all_to_all x0 -> x9, waiting for transfers between devices: none -> 76.3 us  [whole_rows(): lax.all_to_all(jnp.stack([hidden] * lax.axis_size('tensor')), 'tensor', 0...]
    all_to_all x0 -> x9, starting transfers between devices: none -> 31.8 us  [whole_rows(): lax.all_to_all(jnp.stack([hidden] * lax.axis_size('tensor')), 'tensor', 0...]
    another operation x16 -> x25, other arithmetic: 3 us -> 22.1 us  [the longest x9 19.1 us: whole_rows(): jnp.stack([hidden] * lax.axis_size('tensor'))]
  transfers between devices with their start and end apart: 18 -> 27, of which waited for: 18 -> 27; matrix products, arithmetic and copies ran while one was open for 2% -> 4% of each run, Pallas kernels for 0% -> 0%
where the time goes in v1:
time: 865 us; the launch traced here: 864 us
  waiting for transfers between devices  402 us (46%)
  matrix products  177 us (20%)
  blocking collectives  107 us (12%)
  other arithmetic  70.5 us (8%)
  local copies, waits for them, and re-layouts  45.3 us (5%)
  starting transfers between devices  44.4 us (5%)
  between operations  16.2 us (2%)
    reduce_scatter x8, waiting for transfers between devices, section_block(): lax.psum_scatter(partial_out.astype(jnp.bfloat16), 'tensor', scatter_dime...  140 us
    dot_general x8, matrix products, section_block(): projected = jnp.dot(normed, w_in, preferred_element_type=jnp.float32)  83.1 us
    all_to_all x9, waiting for transfers between devices, whole_rows(): lax.all_to_all(jnp.stack([hidden] * lax.axis_size('tensor')), 'tensor', 0...  76.3 us
    dot_general x8, matrix products, section_block(): partial_out = jnp.dot(mixed, out_proj, preferred_element_type=jnp.float32)  76.2 us
    ppermute x8, waiting for transfers between devices, passed_along(): return lax.ppermute(block, axis, route)  73.6 us
    psum x1, waiting for transfers between devices, shards(): lax.psum(class_total.astype(jnp.bfloat16), ('dp', 'pipe'))  58 us
    reduce_scatter x1, waiting for transfers between devices, shards(): lax.psum_scatter(picked.astype(jnp.float32).astype(jnp.bfloat16), ('dp',...  53.6 us
    all_gather x1, blocking collectives, shards(): lax.all_gather(support_tokens, ('dp', 'pipe'), axis=0, tiled=True)  33 us
  transfers between devices with their start and end apart: 27, of which 27 were waited for; matrix products, arithmetic and copies ran while one was open for 4% of the time, Pallas kernels for 0%

profile of v1, /device:TPU:8, one launch (start us, length us, event | category | flops | bytes accessed | tf_op | source)
XLA Modules:
  0.0 863.8 jit_solution(1801952941537797524)
XLA Ops:
  7.2 29.0 %all-gather.1 = s32[16,1,32]{2,1,0:T(1,128)S(1)} all-gather(s32[1,1,32]{2,1,0:T(1,128)} %bitcast.137), channel_id=1, replica_groups=mesh['dp'=4,'pipe'=4,'tensor'=2] {'dp','pipe'}, dimensions={0}, use_global_device_ids=true | all-gather | bytes 2176 | tf_op jit(solution)/shard_map/all_gather | solution.py:74
  36.2 33.0 %all-gather = s32[16,2,32]{2,1,0:T(2,128)S(1)} all-gather(s32[1,2,32]{2,1,0:T(2,128)} %bitcast.133), channel_id=1, replica_groups=mesh['dp'=4,'pipe'=4,'tensor'=2] {'dp','pipe'}, dimensions={0}, use_global_device_ids=true | all-gather | bytes 4352 | tf_op jit(solution)/shard_map/all_gather | solution.py:73
  69.7 20.5 %gather_fusion = bf16[1536,2048]{1,0:T(8,128)(2,1)} fusion(bf16[4008,2048]{1,0:T(8,128)(2,1)} %param.21, s32[2048]{0:T(1024)S(1)} %pad_clamp_fusion), kind=kCustom, calls=%fused_computation | custom fusion | bytes 12589056 | tf_op jit(solution)/shard_map/jit(_take)/gather | solution.py:83
  108.0 18.6 %pad_maximum_fusion.1 = bf16[4096,3072]{1,0:T(8,128)(2,1)} fusion(bf16[4096,512]{1,0:T(8,128)(2,1)} %bitcast.123, bf16[4096,512]{1,0:T(8,128)(2,1)} %bitcast.124, bf16[4096,2048]{1,0:T(8,128)(2,1)} %bitcast.118), kind=kLoop, calls=%fused_computation.54 | loop fusion | flops 75497472 | bytes 50331648 | tf_op jit(solution)/shard_map/concatenate | solution.py:100
  126.7 53.6 %reduce-scatter.3.cloned.1.call-done = bf16[96,2048]{1,0:T(8,128)(2,1)} async-done(((bf16[1536,2048]{1,0:T(8,128)(2,1)}), bf16[96,2048]{1,0:T(8,128)(2,1)}) %reduce-scatter.3.cloned.1.call-update) | async-done | bytes 393232 | tf_op jit(solution)/shard_map/reduce_scatter | solution.py:85
  180.3 560.5 %while.16 = (s32[]{:T(128)}, bf16[96,2048]{1,0:T(8,128)(2,1)}, s32[]{:T(128)}, f32[1,4096]{1,0:T(1,128)S(1)}, bf16[4096,3072]{1,0:T(8,128)(2,1)}, /*index=5*/s32...) while((s32[]{:T(128)}, bf16[96,2048]{1,0:T(8,128)(2,1)}, ...), condition=%wide.region_6.7_spmd.clone, body=%wide.region_1.0_spmd.clone.sunk | while | flops 4072398336 | bytes 75261856 | solution.py:154
  187.7 8.6 all-to-all-done
  196.9 10.4 %fusion.85 = f32[96,3072]{1,0:T(8,128)S(1)} fusion(bf16[4096,3072]{1,0:T(8,128)(2,1)} %get-tuple-element.427, f32[96,4096]{1,0:T(8,128)S(1)} %bitcast.114, f32[4096]{0:T(1024)S(1)} %bitcast.128, f32[96]{0:T(128)S(1)} %add_rsqrt_fusion.3), kind=kOutput, calls=%fused_computation.16.clone.1 | convolution fusion | flops 2417098752 | bytes 27935104 | tf_op jit(solution)/shard_map/while/body/eval_jaxpr/dot_general | solution.py:108
  210.9 9.5 %convolution_convert_fusion.4 = bf16[96,4096]{1,0:T(8,128)(2,1)} fusion(bf16[96,2048]{1,0:T(8,128)(2,1)S(1)} %reshape.350, bf16[2048,4096]{1,0:T(8,128)(2,1)} %get-tuple-element.431), kind=kOutput, calls=%fused_computation.4.clone.1 | convolution fusion | flops 1611005952 | bytes 17956864 | tf_op jit(solution)/shard_map/while/body/eval_jaxpr/dot_general | solution.py:134
  220.5 16.7 %reduce-scatter.5.cloned.1.call-done = bf16[96,2048]{1,0:T(8,128)(2,1)} async-done(((bf16[96,4096]{1,0:T(8,128)(2,1)}), bf16[96,2048]{1,0:T(8,128)(2,1)}) %reduce-scatter.5.cloned.1.call-update) | async-done | bytes 393232 | tf_op jit(solution)/shard_map/while/body/eval_jaxpr/reduce_scatter | solution.py:135
  239.9 9.2 %collective-permute-done = bf16[96,2048]{1,0:T(8,128)(2,1)S(1)} collective-permute-done((bf16[96,2048]{1,0:T(8,128)(2,1)S(1)}, bf16[96,2048]{1,0:T(8,128)(2,1)S(1)}, u32[]{:S(2)}, u32[]{:S(2)}) %collective-permute-start) | collective-permute-done | bytes 393248 | tf_op jit(solution)/shard_map/while/body/eval_jaxpr/ppermute | solution.py:18
  257.2 8.3 all-to-all-done
  266.1 10.4 %fusion.85 = f32[96,3072]{1,0:T(8,128)S(1)} fusion(bf16[4096,3072]{1,0:T(8,128)(2,1)} %get-tuple-element.427, f32[96,4096]{1,0:T(8,128)S(1)} %bitcast.114, f32[4096]{0:T(1024)S(1)} %bitcast.128, f32[96]{0:T(128)S(1)} %add_rsqrt_fusion.3), kind=kOutput, calls=%fused_computation.16.clone.1 | convolution fusion | flops 2417098752 | bytes 27935104 | tf_op jit(solution)/shard_map/while/body/eval_jaxpr/dot_general | solution.py:108
  280.1 9.5 %convolution_convert_fusion.4 = bf16[96,4096]{1,0:T(8,128)(2,1)} fusion(bf16[96,2048]{1,0:T(8,128)(2,1)S(1)} %reshape.350, bf16[2048,4096]{1,0:T(8,128)(2,1)} %get-tuple-element.431), kind=kOutput, calls=%fused_computation.4.clone.1 | convolution fusion | flops 1611005952 | bytes 17956864 | tf_op jit(solution)/shard_map/while/body/eval_jaxpr/dot_general | solution.py:134
  289.7 17.6 %reduce-scatter.5.cloned.1.call-done = bf16[96,2048]{1,0:T(8,128)(2,1)} async-done(((bf16[96,4096]{1,0:T(8,128)(2,1)}), bf16[96,2048]{1,0:T(8,128)(2,1)}) %reduce-scatter.5.cloned.1.call-update) | async-done | bytes 393232 | tf_op jit(solution)/shard_map/while/body/eval_jaxpr/reduce_scatter | solution.py:135
  310.0 9.2 %collective-permute-done = bf16[96,2048]{1,0:T(8,128)(2,1)S(1)} collective-permute-done((bf16[96,2048]{1,0:T(8,128)(2,1)S(1)}, bf16[96,2048]{1,0:T(8,128)(2,1)S(1)}, u32[]{:S(2)}, u32[]{:S(2)}) %collective-permute-start) | collective-permute-done | bytes 393248 | tf_op jit(solution)/shard_map/while/body/eval_jaxpr/ppermute | solution.py:18
  327.4 8.3 all-to-all-done
  336.2 10.4 %fusion.85 = f32[96,3072]{1,0:T(8,128)S(1)} fusion(bf16[4096,3072]{1,0:T(8,128)(2,1)} %get-tuple-element.427, f32[96,4096]{1,0:T(8,128)S(1)} %bitcast.114, f32[4096]{0:T(1024)S(1)} %bitcast.128, f32[96]{0:T(128)S(1)} %add_rsqrt_fusion.3), kind=kOutput, calls=%fused_computation.16.clone.1 | convolution fusion | flops 2417098752 | bytes 27935104 | tf_op jit(solution)/shard_map/while/body/eval_jaxpr/dot_general | solution.py:108
  350.2 9.5 %convolution_convert_fusion.4 = bf16[96,4096]{1,0:T(8,128)(2,1)} fusion(bf16[96,2048]{1,0:T(8,128)(2,1)S(1)} %reshape.350, bf16[2048,4096]{1,0:T(8,128)(2,1)} %get-tuple-element.431), kind=kOutput, calls=%fused_computation.4.clone.1 | convolution fusion | flops 1611005952 | bytes 17956864 | tf_op jit(solution)/shard_map/while/body/eval_jaxpr/dot_general | solution.py:134
  359.8 17.6 %reduce-scatter.5.cloned.1.call-done = bf16[96,2048]{1,0:T(8,128)(2,1)} async-done(((bf16[96,4096]{1,0:T(8,128)(2,1)}), bf16[96,2048]{1,0:T(8,128)(2,1)}) %reduce-scatter.5.cloned.1.call-update) | async-done | bytes 393232 | tf_op jit(solution)/shard_map/while/body/eval_jaxpr/reduce_scatter | solution.py:135
  380.1 9.2 %collective-permute-done = bf16[96,2048]{1,0:T(8,128)(2,1)S(1)} collective-permute-done((bf16[96,2048]{1,0:T(8,128)(2,1)S(1)}, bf16[96,2048]{1,0:T(8,128)(2,1)S(1)}, u32[]{:S(2)}, u32[]{:S(2)}) %collective-permute-start) | collective-permute-done | bytes 393248 | tf_op jit(solution)/shard_map/while/body/eval_jaxpr/ppermute | solution.py:18
  397.5 8.3 all-to-all-done
  406.4 10.4 %fusion.85 = f32[96,3072]{1,0:T(8,128)S(1)} fusion(bf16[4096,3072]{1,0:T(8,128)(2,1)} %get-tuple-element.427, f32[96,4096]{1,0:T(8,128)S(1)} %bitcast.114, f32[4096]{0:T(1024)S(1)} %bitcast.128, f32[96]{0:T(128)S(1)} %add_rsqrt_fusion.3), kind=kOutput, calls=%fused_computation.16.clone.1 | convolution fusion | flops 2417098752 | bytes 27935104 | tf_op jit(solution)/shard_map/while/body/eval_jaxpr/dot_general | solution.py:108
  420.4 9.5 %convolution_convert_fusion.4 = bf16[96,4096]{1,0:T(8,128)(2,1)} fusion(bf16[96,2048]{1,0:T(8,128)(2,1)S(1)} %reshape.350, bf16[2048,4096]{1,0:T(8,128)(2,1)} %get-tuple-element.431), kind=kOutput, calls=%fused_computation.4.clone.1 | convolution fusion | flops 1611005952 | bytes 17956864 | tf_op jit(solution)/shard_map/while/body/eval_jaxpr/dot_general | solution.py:134
  430.0 17.6 %reduce-scatter.5.cloned.1.call-done = bf16[96,2048]{1,0:T(8,128)(2,1)} async-done(((bf16[96,4096]{1,0:T(8,128)(2,1)}), bf16[96,2048]{1,0:T(8,128)(2,1)}) %reduce-scatter.5.cloned.1.call-update) | async-done | bytes 393232 | tf_op jit(solution)/shard_map/while/body/eval_jaxpr/reduce_scatter | solution.py:135
  450.3 9.2 %collective-permute-done = bf16[96,2048]{1,0:T(8,128)(2,1)S(1)} collective-permute-done((bf16[96,2048]{1,0:T(8,128)(2,1)S(1)}, bf16[96,2048]{1,0:T(8,128)(2,1)S(1)}, u32[]{:S(2)}, u32[]{:S(2)}) %collective-permute-start) | collective-permute-done | bytes 393248 | tf_op jit(solution)/shard_map/while/body/eval_jaxpr/ppermute | solution.py:18
  467.6 8.3 all-to-all-done
  476.5 10.4 %fusion.85 = f32[96,3072]{1,0:T(8,128)S(1)} fusion(bf16[4096,3072]{1,0:T(8,128)(2,1)} %get-tuple-element.427, f32[96,4096]{1,0:T(8,128)S(1)} %bitcast.114, f32[4096]{0:T(1024)S(1)} %bitcast.128, f32[96]{0:T(128)S(1)} %add_rsqrt_fusion.3), kind=kOutput, calls=%fused_computation.16.clone.1 | convolution fusion | flops 2417098752 | bytes 27935104 | tf_op jit(solution)/shard_map/while/body/eval_jaxpr/dot_general | solution.py:108
  490.5 9.5 %convolution_convert_fusion.4 = bf16[96,4096]{1,0:T(8,128)(2,1)} fusion(bf16[96,2048]{1,0:T(8,128)(2,1)S(1)} %reshape.350, bf16[2048,4096]{1,0:T(8,128)(2,1)} %get-tuple-element.431), kind=kOutput, calls=%fused_computation.4.clone.1 | convolution fusion | flops 1611005952 | bytes 17956864 | tf_op jit(solution)/shard_map/while/body/eval_jaxpr/dot_general | solution.py:134
  500.1 17.7 %reduce-scatter.5.cloned.1.call-done = bf16[96,2048]{1,0:T(8,128)(2,1)} async-done(((bf16[96,4096]{1,0:T(8,128)(2,1)}), bf16[96,2048]{1,0:T(8,128)(2,1)}) %reduce-scatter.5.cloned.1.call-update) | async-done | bytes 393232 | tf_op jit(solution)/shard_map/while/body/eval_jaxpr/reduce_scatter | solution.py:135
  520.4 9.2 %collective-permute-done = bf16[96,2048]{1,0:T(8,128)(2,1)S(1)} collective-permute-done((bf16[96,2048]{1,0:T(8,128)(2,1)S(1)}, bf16[96,2048]{1,0:T(8,128)(2,1)S(1)}, u32[]{:S(2)}, u32[]{:S(2)}) %collective-permute-start) | collective-permute-done | bytes 393248 | tf_op jit(solution)/shard_map/while/body/eval_jaxpr/ppermute | solution.py:18
  537.8 8.3 all-to-all-done
  546.6 10.4 %fusion.85 = f32[96,3072]{1,0:T(8,128)S(1)} fusion(bf16[4096,3072]{1,0:T(8,128)(2,1)} %get-tuple-element.427, f32[96,4096]{1,0:T(8,128)S(1)} %bitcast.114, f32[4096]{0:T(1024)S(1)} %bitcast.128, f32[96]{0:T(128)S(1)} %add_rsqrt_fusion.3), kind=kOutput, calls=%fused_computation.16.clone.1 | convolution fusion | flops 2417098752 | bytes 27935104 | tf_op jit(solution)/shard_map/while/body/eval_jaxpr/dot_general | solution.py:108
  560.6 9.5 %convolution_convert_fusion.4 = bf16[96,4096]{1,0:T(8,128)(2,1)} fusion(bf16[96,2048]{1,0:T(8,128)(2,1)S(1)} %reshape.350, bf16[2048,4096]{1,0:T(8,128)(2,1)} %get-tuple-element.431), kind=kOutput, calls=%fused_computation.4.clone.1 | convolution fusion | flops 1611005952 | bytes 17956864 | tf_op jit(solution)/shard_map/while/body/eval_jaxpr/dot_general | solution.py:134
  570.2 17.6 %reduce-scatter.5.cloned.1.call-done = bf16[96,2048]{1,0:T(8,128)(2,1)} async-done(((bf16[96,4096]{1,0:T(8,128)(2,1)}), bf16[96,2048]{1,0:T(8,128)(2,1)}) %reduce-scatter.5.cloned.1.call-update) | async-done | bytes 393232 | tf_op jit(solution)/shard_map/while/body/eval_jaxpr/reduce_scatter | solution.py:135
  590.5 9.2 %collective-permute-done = bf16[96,2048]{1,0:T(8,128)(2,1)S(1)} collective-permute-done((bf16[96,2048]{1,0:T(8,128)(2,1)S(1)}, bf16[96,2048]{1,0:T(8,128)(2,1)S(1)}, u32[]{:S(2)}, u32[]{:S(2)}) %collective-permute-start) | collective-permute-done | bytes 393248 | tf_op jit(solution)/shard_map/while/body/eval_jaxpr/ppermute | solution.py:18
  607.9 8.3 all-to-all-done
  616.8 10.4 %fusion.85 = f32[96,3072]{1,0:T(8,128)S(1)} fusion(bf16[4096,3072]{1,0:T(8,128)(2,1)} %get-tuple-element.427, f32[96,4096]{1,0:T(8,128)S(1)} %bitcast.114, f32[4096]{0:T(1024)S(1)} %bitcast.128, f32[96]{0:T(128)S(1)} %add_rsqrt_fusion.3), kind=kOutput, calls=%fused_computation.16.clone.1 | convolution fusion | flops 2417098752 | bytes 27935104 | tf_op jit(solution)/shard_map/while/body/eval_jaxpr/dot_general | solution.py:108
  630.8 9.5 %convolution_convert_fusion.4 = bf16[96,4096]{1,0:T(8,128)(2,1)} fusion(bf16[96,2048]{1,0:T(8,128)(2,1)S(1)} %reshape.350, bf16[2048,4096]{1,0:T(8,128)(2,1)} %get-tuple-element.431), kind=kOutput, calls=%fused_computation.4.clone.1 | convolution fusion | flops 1611005952 | bytes 17956864 | tf_op jit(solution)/shard_map/while/body/eval_jaxpr/dot_general | solution.py:134
  640.3 17.7 %reduce-scatter.5.cloned.1.call-done = bf16[96,2048]{1,0:T(8,128)(2,1)} async-done(((bf16[96,4096]{1,0:T(8,128)(2,1)}), bf16[96,2048]{1,0:T(8,128)(2,1)}) %reduce-scatter.5.cloned.1.call-update) | async-done | bytes 393232 | tf_op jit(solution)/shard_map/while/body/eval_jaxpr/reduce_scatter | solution.py:135
  660.7 9.2 %collective-permute-done = bf16[96,2048]{1,0:T(8,128)(2,1)S(1)} collective-permute-done((bf16[96,2048]{1,0:T(8,128)(2,1)S(1)}, bf16[96,2048]{1,0:T(8,128)(2,1)S(1)}, u32[]{:S(2)}, u32[]{:S(2)}) %collective-permute-start) | collective-permute-done | bytes 393248 | tf_op jit(solution)/shard_map/while/body/eval_jaxpr/ppermute | solution.py:18
  686.9 10.4 %fusion.85 = f32[96,3072]{1,0:T(8,128)S(1)} fusion(bf16[4096,3072]{1,0:T(8,128)(2,1)} %get-tuple-element.427, f32[96,4096]{1,0:T(8,128)S(1)} %bitcast.114, f32[4096]{0:T(1024)S(1)} %bitcast.128, f32[96]{0:T(128)S(1)} %add_rsqrt_fusion.3), kind=kOutput, calls=%fused_computation.16.clone.1 | convolution fusion | flops 2417098752 | bytes 27935104 | tf_op jit(solution)/shard_map/while/body/eval_jaxpr/dot_general | solution.py:108
  700.9 9.5 %convolution_convert_fusion.4 = bf16[96,4096]{1,0:T(8,128)(2,1)} fusion(bf16[96,2048]{1,0:T(8,128)(2,1)S(1)} %reshape.350, bf16[2048,4096]{1,0:T(8,128)(2,1)} %get-tuple-element.431), kind=kOutput, calls=%fused_computation.4.clone.1 | convolution fusion | flops 1611005952 | bytes 17956864 | tf_op jit(solution)/shard_map/while/body/eval_jaxpr/dot_general | solution.py:134
  710.5 17.7 %reduce-scatter.5.cloned.1.call-done = bf16[96,2048]{1,0:T(8,128)(2,1)} async-done(((bf16[96,4096]{1,0:T(8,128)(2,1)}), bf16[96,2048]{1,0:T(8,128)(2,1)}) %reduce-scatter.5.cloned.1.call-update) | async-done | bytes 393232 | tf_op jit(solution)/shard_map/while/body/eval_jaxpr/reduce_scatter | solution.py:135
  730.9 9.2 %collective-permute-done = bf16[96,2048]{1,0:T(8,128)(2,1)S(1)} collective-permute-done((bf16[96,2048]{1,0:T(8,128)(2,1)S(1)}, bf16[96,2048]{1,0:T(8,128)(2,1)S(1)}, u32[]{:S(2)}, u32[]{:S(2)}) %collective-permute-start) | collective-permute-done | bytes 393248 | tf_op jit(solution)/shard_map/while/body/eval_jaxpr/ppermute | solution.py:18
  746.6 9.8 %all-to-all-done.1 = bf16[2,96,2048]{2,1,0:T(8,128)(2,1)S(1)} async-done(((bf16[2,96,2048]{2,1,0:T(8,128)(2,1)}), bf16[2,96,2048]{2,1,0:T(8,128)(2,1)S(1)}, u32[]{:S(2)}, u32[]{:S(2)}) %all-to-all-start.1) | async-done | bytes 786464 | tf_op jit(solution)/shard_map/all_to_all | solution.py:39
  758.6 32.3 %psum.22 = bf16[32]{0:T(256)(128)(2,1)S(1)} all-reduce(bf16[32]{0:T(256)(128)(2,1)S(1)} %convert_reduce_fusion), channel_id=1, replica_groups=mesh['dp'=4,'pipe'=4,'tensor'=2] {'dp','pipe'}, use_global_device_ids=true, to_apply=%region_11.12 | all-reduce | flops 32 | bytes 128 | tf_op jit(solution)/shard_map/psum | solution.py:172
  791.6 58.0 %all-reduce.5.cloned.1.call-done = bf16[32,2048]{1,0:T(8,128)(2,1)} async-done(((bf16[32,2048]{1,0:T(8,128)(2,1)}), bf16[32,2048]{1,0:T(8,128)(2,1)}) %all-reduce.5.cloned.1.call-update) | async-done | bytes 131088 | tf_op jit(solution)/shard_map/psum | solution.py:171
  (349 shorter events, 159.4 us)
Async XLA Ops:
  7.2 173.2 %reduce-scatter.3.cloned.1.call-start = ((), (), s32[]{:S(2)}) async-start(), calls=%async_computation.4 | async-start | bytes 6684672 | tf_op jit(solution)/shard_map/reduce_scatter | solution.py:85
  97.3 2.1 copy-start.5
  108.0 72.3 %copy-start.2 = (f32[1,4096]{1,0:T(1,128)S(1)}, f32[1,4096]{1,0:T(1,128)}, u32[]{:S(2)}) copy-start(f32[1,4096]{1,0:T(1,128)} %param.22) | copy-start | bytes 49156
  182.5 13.9 %all-to-all-start = ((bf16[2,96,2048]{2,1,0:T(8,128)(2,1)}), bf16[2,96,2048]{2,1,0:T(8,128)(2,1)S(1)}, u32[]{:S(2)}, u32[]{:S(2)}) async-start(bf16[2,96,2048]{2,1,0:T(8,128)(2,1)} %pad_maximum_fusion.4), calls=%async_computation | async-start | bytes 1572864 | tf_op jit(solution)/shard_map/while/body/eval_jaxpr/all_to_all | solution.py:39
  186.0 51.2 %reduce-scatter.5.cloned.1.call-start = ((), (), s32[]{:S(2)}) async-start(), calls=%async_computation.6 | async-start | bytes 1179648 | tf_op jit(solution)/shard_map/while/body/eval_jaxpr/reduce_scatter | solution.py:135
  210.9 26.3 %copy-start = (bf16[96,2048]{1,0:T(8,128)(2,1)S(1)}, bf16[96,2048]{1,0:T(8,128)(2,1)}, u32[]{:S(2)}) copy-start(bf16[96,2048]{1,0:T(8,128)(2,1)} %get-tuple-element.408) | copy-start | bytes 1179652 | tf_op jit(solution)/shard_map/while
  238.3 10.7 %collective-permute-start = (bf16[96,2048]{1,0:T(8,128)(2,1)S(1)}, bf16[96,2048]{1,0:T(8,128)(2,1)S(1)}, u32[]{:S(2)}, u32[]{:S(2)}) collective-permute-start(bf16[96,2048]{1,0:T(8,128)(2,1)S(1)} %fusion.90), channel_id=1, source_target_pairs={{6,0},{0,2},{2,4},{4,6},{7,1},{1,3},{3,5},{5,7},{14,8},{8,10},{10,... | collective-permute-start | bytes 1179656 | tf_op jit(solution)/shard_map/while/body/eval_jaxpr/ppermute | solution.py:18
  249.0 0.8 copy-start.1
  251.9 13.6 %all-to-all-start = ((bf16[2,96,2048]{2,1,0:T(8,128)(2,1)}), bf16[2,96,2048]{2,1,0:T(8,128)(2,1)S(1)}, u32[]{:S(2)}, u32[]{:S(2)}) async-start(bf16[2,96,2048]{2,1,0:T(8,128)(2,1)} %pad_maximum_fusion.4), calls=%async_computation | async-start | bytes 1572864 | tf_op jit(solution)/shard_map/while/body/eval_jaxpr/all_to_all | solution.py:39
  255.5 51.8 %reduce-scatter.5.cloned.1.call-start = ((), (), s32[]{:S(2)}) async-start(), calls=%async_computation.6 | async-start | bytes 1179648 | tf_op jit(solution)/shard_map/while/body/eval_jaxpr/reduce_scatter | solution.py:135
  280.1 27.2 %copy-start = (bf16[96,2048]{1,0:T(8,128)(2,1)S(1)}, bf16[96,2048]{1,0:T(8,128)(2,1)}, u32[]{:S(2)}) copy-start(bf16[96,2048]{1,0:T(8,128)(2,1)} %get-tuple-element.408) | copy-start | bytes 1179652 | tf_op jit(solution)/shard_map/while
  308.4 10.8 %collective-permute-start = (bf16[96,2048]{1,0:T(8,128)(2,1)S(1)}, bf16[96,2048]{1,0:T(8,128)(2,1)S(1)}, u32[]{:S(2)}, u32[]{:S(2)}) collective-permute-start(bf16[96,2048]{1,0:T(8,128)(2,1)S(1)} %fusion.90), channel_id=1, source_target_pairs={{6,0},{0,2},{2,4},{4,6},{7,1},{1,3},{3,5},{5,7},{14,8},{8,10},{10,... | collective-permute-start | bytes 1179656 | tf_op jit(solution)/shard_map/while/body/eval_jaxpr/ppermute | solution.py:18
  319.2 0.8 copy-start.1
  322.1 13.6 %all-to-all-start = ((bf16[2,96,2048]{2,1,0:T(8,128)(2,1)}), bf16[2,96,2048]{2,1,0:T(8,128)(2,1)S(1)}, u32[]{:S(2)}, u32[]{:S(2)}) async-start(bf16[2,96,2048]{2,1,0:T(8,128)(2,1)} %pad_maximum_fusion.4), calls=%async_computation | async-start | bytes 1572864 | tf_op jit(solution)/shard_map/while/body/eval_jaxpr/all_to_all | solution.py:39
  325.6 51.8 %reduce-scatter.5.cloned.1.call-start = ((), (), s32[]{:S(2)}) async-start(), calls=%async_computation.6 | async-start | bytes 1179648 | tf_op jit(solution)/shard_map/while/body/eval_jaxpr/reduce_scatter | solution.py:135
  350.2 27.2 %copy-start = (bf16[96,2048]{1,0:T(8,128)(2,1)S(1)}, bf16[96,2048]{1,0:T(8,128)(2,1)}, u32[]{:S(2)}) copy-start(bf16[96,2048]{1,0:T(8,128)(2,1)} %get-tuple-element.408) | copy-start | bytes 1179652 | tf_op jit(solution)/shard_map/while
  378.6 10.7 %collective-permute-start = (bf16[96,2048]{1,0:T(8,128)(2,1)S(1)}, bf16[96,2048]{1,0:T(8,128)(2,1)S(1)}, u32[]{:S(2)}, u32[]{:S(2)}) collective-permute-start(bf16[96,2048]{1,0:T(8,128)(2,1)S(1)} %fusion.90), channel_id=1, source_target_pairs={{6,0},{0,2},{2,4},{4,6},{7,1},{1,3},{3,5},{5,7},{14,8},{8,10},{10,... | collective-permute-start | bytes 1179656 | tf_op jit(solution)/shard_map/while/body/eval_jaxpr/ppermute | solution.py:18
  389.3 0.8 copy-start.1
  392.2 13.6 %all-to-all-start = ((bf16[2,96,2048]{2,1,0:T(8,128)(2,1)}), bf16[2,96,2048]{2,1,0:T(8,128)(2,1)S(1)}, u32[]{:S(2)}, u32[]{:S(2)}) async-start(bf16[2,96,2048]{2,1,0:T(8,128)(2,1)} %pad_maximum_fusion.4), calls=%async_computation | async-start | bytes 1572864 | tf_op jit(solution)/shard_map/while/body/eval_jaxpr/all_to_all | solution.py:39
  395.8 51.8 %reduce-scatter.5.cloned.1.call-start = ((), (), s32[]{:S(2)}) async-start(), calls=%async_computation.6 | async-start | bytes 1179648 | tf_op jit(solution)/shard_map/while/body/eval_jaxpr/reduce_scatter | solution.py:135
  420.4 27.2 %copy-start = (bf16[96,2048]{1,0:T(8,128)(2,1)S(1)}, bf16[96,2048]{1,0:T(8,128)(2,1)}, u32[]{:S(2)}) copy-start(bf16[96,2048]{1,0:T(8,128)(2,1)} %get-tuple-element.408) | copy-start | bytes 1179652 | tf_op jit(solution)/shard_map/while
  448.7 10.7 %collective-permute-start = (bf16[96,2048]{1,0:T(8,128)(2,1)S(1)}, bf16[96,2048]{1,0:T(8,128)(2,1)S(1)}, u32[]{:S(2)}, u32[]{:S(2)}) collective-permute-start(bf16[96,2048]{1,0:T(8,128)(2,1)S(1)} %fusion.90), channel_id=1, source_target_pairs={{6,0},{0,2},{2,4},{4,6},{7,1},{1,3},{3,5},{5,7},{14,8},{8,10},{10,... | collective-permute-start | bytes 1179656 | tf_op jit(solution)/shard_map/while/body/eval_jaxpr/ppermute | solution.py:18
  459.5 0.8 copy-start.1
  462.4 13.6 %all-to-all-start = ((bf16[2,96,2048]{2,1,0:T(8,128)(2,1)}), bf16[2,96,2048]{2,1,0:T(8,128)(2,1)S(1)}, u32[]{:S(2)}, u32[]{:S(2)}) async-start(bf16[2,96,2048]{2,1,0:T(8,128)(2,1)} %pad_maximum_fusion.4), calls=%async_computation | async-start | bytes 1572864 | tf_op jit(solution)/shard_map/while/body/eval_jaxpr/all_to_all | solution.py:39
  465.9 51.9 %reduce-scatter.5.cloned.1.call-start = ((), (), s32[]{:S(2)}) async-start(), calls=%async_computation.6 | async-start | bytes 1179648 | tf_op jit(solution)/shard_map/while/body/eval_jaxpr/reduce_scatter | solution.py:135
  490.5 27.3 %copy-start = (bf16[96,2048]{1,0:T(8,128)(2,1)S(1)}, bf16[96,2048]{1,0:T(8,128)(2,1)}, u32[]{:S(2)}) copy-start(bf16[96,2048]{1,0:T(8,128)(2,1)} %get-tuple-element.408) | copy-start | bytes 1179652 | tf_op jit(solution)/shard_map/while
  518.9 10.7 %collective-permute-start = (bf16[96,2048]{1,0:T(8,128)(2,1)S(1)}, bf16[96,2048]{1,0:T(8,128)(2,1)S(1)}, u32[]{:S(2)}, u32[]{:S(2)}) collective-permute-start(bf16[96,2048]{1,0:T(8,128)(2,1)S(1)} %fusion.90), channel_id=1, source_target_pairs={{6,0},{0,2},{2,4},{4,6},{7,1},{1,3},{3,5},{5,7},{14,8},{8,10},{10,... | collective-permute-start | bytes 1179656 | tf_op jit(solution)/shard_map/while/body/eval_jaxpr/ppermute | solution.py:18
  529.6 0.8 copy-start.1
  532.5 13.6 %all-to-all-start = ((bf16[2,96,2048]{2,1,0:T(8,128)(2,1)}), bf16[2,96,2048]{2,1,0:T(8,128)(2,1)S(1)}, u32[]{:S(2)}, u32[]{:S(2)}) async-start(bf16[2,96,2048]{2,1,0:T(8,128)(2,1)} %pad_maximum_fusion.4), calls=%async_computation | async-start | bytes 1572864 | tf_op jit(solution)/shard_map/while/body/eval_jaxpr/all_to_all | solution.py:39
  536.0 51.8 %reduce-scatter.5.cloned.1.call-start = ((), (), s32[]{:S(2)}) async-start(), calls=%async_computation.6 | async-start | bytes 1179648 | tf_op jit(solution)/shard_map/while/body/eval_jaxpr/reduce_scatter | solution.py:135
  560.6 27.2 %copy-start = (bf16[96,2048]{1,0:T(8,128)(2,1)S(1)}, bf16[96,2048]{1,0:T(8,128)(2,1)}, u32[]{:S(2)}) copy-start(bf16[96,2048]{1,0:T(8,128)(2,1)} %get-tuple-element.408) | copy-start | bytes 1179652 | tf_op jit(solution)/shard_map/while
  589.0 10.7 %collective-permute-start = (bf16[96,2048]{1,0:T(8,128)(2,1)S(1)}, bf16[96,2048]{1,0:T(8,128)(2,1)S(1)}, u32[]{:S(2)}, u32[]{:S(2)}) collective-permute-start(bf16[96,2048]{1,0:T(8,128)(2,1)S(1)} %fusion.90), channel_id=1, source_target_pairs={{6,0},{0,2},{2,4},{4,6},{7,1},{1,3},{3,5},{5,7},{14,8},{8,10},{10,... | collective-permute-start | bytes 1179656 | tf_op jit(solution)/shard_map/while/body/eval_jaxpr/ppermute | solution.py:18
  599.7 0.8 copy-start.1
  602.6 13.6 %all-to-all-start = ((bf16[2,96,2048]{2,1,0:T(8,128)(2,1)}), bf16[2,96,2048]{2,1,0:T(8,128)(2,1)S(1)}, u32[]{:S(2)}, u32[]{:S(2)}) async-start(bf16[2,96,2048]{2,1,0:T(8,128)(2,1)} %pad_maximum_fusion.4), calls=%async_computation | async-start | bytes 1572864 | tf_op jit(solution)/shard_map/while/body/eval_jaxpr/all_to_all | solution.py:39
  606.2 51.9 %reduce-scatter.5.cloned.1.call-start = ((), (), s32[]{:S(2)}) async-start(), calls=%async_computation.6 | async-start | bytes 1179648 | tf_op jit(solution)/shard_map/while/body/eval_jaxpr/reduce_scatter | solution.py:135
  630.8 27.3 %copy-start = (bf16[96,2048]{1,0:T(8,128)(2,1)S(1)}, bf16[96,2048]{1,0:T(8,128)(2,1)}, u32[]{:S(2)}) copy-start(bf16[96,2048]{1,0:T(8,128)(2,1)} %get-tuple-element.408) | copy-start | bytes 1179652 | tf_op jit(solution)/shard_map/while
  659.2 10.7 %collective-permute-start = (bf16[96,2048]{1,0:T(8,128)(2,1)S(1)}, bf16[96,2048]{1,0:T(8,128)(2,1)S(1)}, u32[]{:S(2)}, u32[]{:S(2)}) collective-permute-start(bf16[96,2048]{1,0:T(8,128)(2,1)S(1)} %fusion.90), channel_id=1, source_target_pairs={{6,0},{0,2},{2,4},{4,6},{7,1},{1,3},{3,5},{5,7},{14,8},{8,10},{10,... | collective-permute-start | bytes 1179656 | tf_op jit(solution)/shard_map/while/body/eval_jaxpr/ppermute | solution.py:18
  669.9 0.8 copy-start.1
  672.8 13.5 %all-to-all-start = ((bf16[2,96,2048]{2,1,0:T(8,128)(2,1)}), bf16[2,96,2048]{2,1,0:T(8,128)(2,1)S(1)}, u32[]{:S(2)}, u32[]{:S(2)}) async-start(bf16[2,96,2048]{2,1,0:T(8,128)(2,1)} %pad_maximum_fusion.4), calls=%async_computation | async-start | bytes 1572864 | tf_op jit(solution)/shard_map/while/body/eval_jaxpr/all_to_all | solution.py:39
  676.3 51.9 %reduce-scatter.5.cloned.1.call-start = ((), (), s32[]{:S(2)}) async-start(), calls=%async_computation.6 | async-start | bytes 1179648 | tf_op jit(solution)/shard_map/while/body/eval_jaxpr/reduce_scatter | solution.py:135
  700.9 27.3 %copy-start = (bf16[96,2048]{1,0:T(8,128)(2,1)S(1)}, bf16[96,2048]{1,0:T(8,128)(2,1)}, u32[]{:S(2)}) copy-start(bf16[96,2048]{1,0:T(8,128)(2,1)} %get-tuple-element.408) | copy-start | bytes 1179652 | tf_op jit(solution)/shard_map/while
  729.3 10.7 %collective-permute-start = (bf16[96,2048]{1,0:T(8,128)(2,1)S(1)}, bf16[96,2048]{1,0:T(8,128)(2,1)S(1)}, u32[]{:S(2)}, u32[]{:S(2)}) collective-permute-start(bf16[96,2048]{1,0:T(8,128)(2,1)S(1)} %fusion.90), channel_id=1, source_target_pairs={{6,0},{0,2},{2,4},{4,6},{7,1},{1,3},{3,5},{5,7},{14,8},{8,10},{10,... | collective-permute-start | bytes 1179656 | tf_op jit(solution)/shard_map/while/body/eval_jaxpr/ppermute | solution.py:18
  740.0 0.8 copy-start.1
  740.8 16.6 %copy-start.4 = (s32[2,1]{0,1:T(1,128)S(1)}, s32[2,1]{0,1:T(1,128)}, u32[]{:S(2)}) copy-start(s32[2,1]{0,1:T(1,128)} %param.17) | copy-start | bytes 28
  742.9 13.5 %all-to-all-start.1 = ((bf16[2,96,2048]{2,1,0:T(8,128)(2,1)}), bf16[2,96,2048]{2,1,0:T(8,128)(2,1)S(1)}, u32[]{:S(2)}, u32[]{:S(2)}) async-start(bf16[2,96,2048]{2,1,0:T(8,128)(2,1)} %pad_maximum_fusion.2), calls=%async_computation.3 | async-start | bytes 1572864 | tf_op jit(solution)/shard_map/all_to_all | solution.py:39
  746.4 103.2 %all-reduce.5.cloned.1.call-start = ((), (), s32[]{:S(2)}) async-start(), calls=%async_computation.5 | async-start | bytes 262144 | tf_op jit(solution)/shard_map/psum | solution.py:171
  746.5 10.5 %dynamic-slice-start = ((f32[4096]{0:T(1024)}, s32[]{:T(128)}), f32[2048]{0:T(1024)S(1)}, s32[]{:S(2)}) async-start(f32[4096]{0:T(1024)} %param.27, s32[]{:T(128)} %select_n.115), calls=%async_computation.7 | async-start | bytes 16896 | tf_op jit(solution)/shard_map/dynamic_slice | solution.py:155
  850.7 6.3 copy-start.3
  (1 other events, 0.7 us)
Sparse Core Ops, SparseCore 0:
  97.4 82.8 reduce-scatter.2
  220.6 16.5 reduce-scatter.4
  289.8 17.4 reduce-scatter.4
  359.9 17.4 reduce-scatter.4
  430.1 17.4 reduce-scatter.4
  500.2 17.5 reduce-scatter.4
  570.3 17.5 reduce-scatter.4
  640.4 17.5 reduce-scatter.4
  710.6 17.5 reduce-scatter.4
  758.6 90.9 all-reduce.4
